TPU v7x, 32 devices: a whole 2x2x4 slice. The times are simulated.
32 devices in a mesh: aa: 8 (over z, x), ba: 4 (over y, core).
Axes of the slice: x: 2, y: 2, z: 4, core: 2. Of those that a mesh axis runs over, the one named last changes fastest.
Arguments:
- grid_features: bfloat16 [128, 128, 256, 128], P('aa', 'ba'), may hold values from -6 to 6
- weight_real: bfloat16 [32, 32, 16, 128, 128], P('ba', None, 'aa'), may hold values from -6 to 6
- weight_imag: bfloat16 [32, 32, 16, 128, 128], P('ba', None, 'aa'), may hold values from -6 to 6
- mode_keep: int32 [32, 16], P('ba', 'aa'), may hold values from 1 to 16, as said below
- local_weight: bfloat16 [128, 128], replicated, may hold values from -0.5 to 0.5
- local_bias: bfloat16 [128], replicated, may hold values from -3 to 3
Outputs:
- layer_output: bfloat16 [128, 128, 256, 128], P('aa', 'ba')
Inputs may be any that keep to these rules, and one draw needn't show every extreme that they name: mode_keep[i, k] counts the retained levels of the second frequency on the line of the i-th retained first frequency and the k-th third frequency.
All inputs are finite; a program needn't handle non-finite values.
Results may differ from a plain program's by a relative error of at most 0.012.
Values may be sent and summed in bfloat16 or wider, within the bound.
A program may use at most 256 MiB of HBM per device.

v0:
```python
import math

import jax
import jax.numpy as jnp
from jax import lax
from jax.sharding import PartitionSpec as P

NX = 128
NY = 128
NZ = 256
KX = 32
KY = 32
KZ = 16


highest = lax.Precision.HIGHEST


def kept_modes(length, number):
    positions = jnp.arange(number, dtype=jnp.int32)
    return jnp.where(positions < number // 2, positions, positions + (length - number))


def phase_tables(length, mode_list):
    places = jnp.arange(length, dtype=jnp.int32)
    phase_steps = places[:, None] * mode_list[None, :] % length
    angles = phase_steps.astype(jnp.float32) * (2.0 * math.pi / length)
    return (jnp.cos(angles), jnp.sin(angles))


def forward_kernel(length, number):
    cosine_table, sine_table = phase_tables(length, kept_modes(length, number))
    upper_rows = jnp.concatenate([cosine_table, -sine_table], axis=1)
    lower_rows = jnp.concatenate([sine_table, cosine_table], axis=1)
    return jnp.concatenate([upper_rows, lower_rows], axis=0)


def inverse_kernel(length, number):
    cosine_table, sine_table = phase_tables(length, kept_modes(length, number))
    upper_rows = jnp.concatenate([cosine_table.T, sine_table.T], axis=1)
    lower_rows = jnp.concatenate([-sine_table.T, cosine_table.T], axis=1)
    return jnp.concatenate([upper_rows, lower_rows], axis=0)


def depth_kernels():
    cosine_table, sine_table = phase_tables(NZ, jnp.arange(KZ, dtype=jnp.int32))
    forward = jnp.concatenate([cosine_table, -sine_table], axis=1).astype(jnp.bfloat16)
    factor = jnp.where(jnp.arange(KZ, dtype=jnp.int32) == 0, 1.0, 2.0).astype(jnp.float32) / (
        NX * NY * NZ
    )
    inverse = jnp.concatenate(
        [cosine_table.T * factor[:, None], -sine_table.T * factor[:, None]], axis=0
    ).astype(jnp.bfloat16)
    return (forward, inverse)


def along_first(operand, kernel):
    return jnp.einsum(
        "pabc,pq->qabc", operand, kernel, precision=highest, preferred_element_type=jnp.float32
    )


def along_second(operand, kernel):
    return jnp.einsum(
        "apbc,pq->aqbc", operand, kernel, precision=highest, preferred_element_type=jnp.float32
    )


def mode_mask(kept_counts):
    positions = jnp.arange(KY, dtype=jnp.int32)
    levels = jnp.where(positions < KY // 2, positions, KY - 1 - positions)
    return (levels[None, :, None] < kept_counts[:, None, :]).astype(jnp.float32)


def mix_modes(spec_real, spec_imag, weight_real, weight_imag, kept_counts):
    pattern = "abcd,abcde->abce"
    out_real = jnp.einsum(
        pattern, spec_real, weight_real, preferred_element_type=jnp.float32
    ) - jnp.einsum(pattern, spec_imag, weight_imag, preferred_element_type=jnp.float32)
    out_imag = jnp.einsum(
        pattern, spec_real, weight_imag, preferred_element_type=jnp.float32
    ) + jnp.einsum(pattern, spec_imag, weight_real, preferred_element_type=jnp.float32)
    keep_mask = mode_mask(kept_counts)[..., None]
    return (out_real * keep_mask, out_imag * keep_mask)


def per_device(grid_features, weight_real, weight_imag, mode_keep, local_weight, local_bias):
    forward_depth, inverse_depth = depth_kernels()
    coeffs = jnp.einsum(
        "xyzc,zk->xykc", grid_features, forward_depth, preferred_element_type=jnp.float32
    ).astype(jnp.bfloat16)
    depth_real = coeffs[:, :, :KZ]
    depth_imag = coeffs[:, :, KZ:]
    gathered = (
        lax.all_to_all(depth_real, "aa", split_axis=2, concat_axis=0, tiled=True),
        lax.all_to_all(depth_imag, "aa", split_axis=2, concat_axis=0, tiled=True),
    )
    result = along_first(
        jnp.concatenate(gathered, axis=0).astype(jnp.float32), forward_kernel(NX, KX)
    )
    gathered = (
        lax.all_to_all(
            result[:KX].astype(jnp.bfloat16), "ba", split_axis=0, concat_axis=1, tiled=True
        ).astype(jnp.float32),
        lax.all_to_all(
            result[KX:].astype(jnp.bfloat16), "ba", split_axis=0, concat_axis=1, tiled=True
        ).astype(jnp.float32),
    )
    result = along_second(jnp.concatenate(gathered, axis=1), forward_kernel(NY, KY)).astype(
        jnp.bfloat16
    )
    mixed_real, mixed_imag = mix_modes(
        result[:, :KY], result[:, KY:], weight_real, weight_imag, mode_keep
    )
    result = along_second(jnp.concatenate([mixed_real, mixed_imag], axis=1), inverse_kernel(NY, KY))
    gathered = (
        lax.all_to_all(
            result[:, :NY].astype(jnp.bfloat16), "ba", split_axis=1, concat_axis=0, tiled=True
        ).astype(jnp.float32),
        lax.all_to_all(
            result[:, NY:].astype(jnp.bfloat16), "ba", split_axis=1, concat_axis=0, tiled=True
        ).astype(jnp.float32),
    )
    result = along_first(jnp.concatenate(gathered, axis=0), inverse_kernel(NX, KX)).astype(
        jnp.bfloat16
    )
    back_field = (
        lax.all_to_all(result[:NX], "aa", split_axis=0, concat_axis=2, tiled=True),
        lax.all_to_all(result[NX:], "aa", split_axis=0, concat_axis=2, tiled=True),
    )
    spectral = jnp.einsum(
        "xykc,kz->xyzc",
        jnp.concatenate(back_field, axis=2),
        inverse_depth,
        preferred_element_type=jnp.float32,
    )
    local_term = jnp.einsum(
        "xyzc,cd->xyzd", grid_features, local_weight, preferred_element_type=jnp.float32
    )
    return jax.nn.gelu(spectral + local_term + local_bias.astype(jnp.float32)).astype(jnp.bfloat16)


def solution(mesh):
    in_specs = (
        P("aa", "ba", None, None),
        P("ba", None, "aa", None, None),
        P("ba", None, "aa", None, None),
        P("ba", "aa"),
        P(),
        P(),
    )
    out_specs = P("aa", "ba", None, None)
    return jax.shard_map(
        per_device, mesh=mesh, in_specs=in_specs, out_specs=out_specs, check_vma=False
    )
```

profile of v0, /device:TPU:0, one launch (start us, length us, event | category | flops | bytes accessed | tf_op | source)
XLA Modules:
  0.0 419.5 jit_solution(7839791159601582577)
XLA Ops:
  0.1 18.5 %convert_bitcast_fusion = bf16[16,32,32,128]{3,2,1,0:T(8,128)(2,1)} fusion(bf16[16,32,256,128]{3,2,1,0:T(8,128)(2,1)} %param.6, bf16[256,16]{0,1:T(8,128)(2,1)S(1)} %get-tuple-element.25, bf16[256,16]{0,1:T(8,128)(2,1)S(1)} %get-tuple-element.26), kind=kOutput, calls=%fused_computation.19 | convolution fusion | flops 1075871744 | bytes 37765120 | tf_op jit(solution)/shard_map/xyzc,zk->xykc/dot_general | solution.py:89
  18.6 4.5 %fusion.87 = (bf16[16,32,16,128]{3,2,1,0:T(8,128)(2,1)S(1)}, bf16[16,32,16,128]{3,2,1,0:T(8,128)(2,1)}) fusion(bf16[16,32,32,128]{3,2,1,0:T(8,128)(2,1)} %convert_bitcast_fusion), kind=kLoop, calls=%fused_computation.122 | loop fusion | bytes 8388608 | tf_op jit(solution)/shard_map/slice | solution.py:92
  25.0 7.3 %all-to-all-start = ((bf16[16,32,16,128]{3,1,0,2:T(8,128)(2,1)}), bf16[16,32,16,128]{3,1,0,2:T(8,128)(2,1)S(1)}, u32[]{:S(2)}, u32[]{:S(2)}) async-start(bf16[16,32,16,128]{3,1,0,2:T(8,128)(2,1)} %copy.16), calls=%async_computation | async-start | bytes 4194304 | tf_op jit(solution)/shard_map/all_to_all | solution.py:95
  32.2 3.5 copy.18
  35.7 44.8 %all-to-all-done = bf16[16,32,16,128]{3,1,0,2:T(8,128)(2,1)S(1)} async-done(((bf16[16,32,16,128]{3,1,0,2:T(8,128)(2,1)}), bf16[16,32,16,128]{3,1,0,2:T(8,128)(2,1)S(1)}, u32[]{:S(2)}, u32[]{:S(2)}) %all-to-all-start) | async-done | bytes 2097184 | tf_op jit(solution)/shard_map/all_to_all | solution.py:95
  80.5 4.4 %all-to-all-start.1 = ((bf16[16,32,16,128]{3,1,0,2:T(8,128)(2,1)}), bf16[16,32,16,128]{3,1,0,2:T(8,128)(2,1)}, u32[]{:S(2)}, u32[]{:S(2)}) async-start(bf16[16,32,16,128]{3,1,0,2:T(8,128)(2,1)} %copy.18), calls=%async_computation.1 | async-start | bytes 4194304 | tf_op jit(solution)/shard_map/all_to_all | solution.py:96
  87.2 45.5 %all-to-all-done.1 = bf16[16,32,16,128]{3,1,0,2:T(8,128)(2,1)} async-done(((bf16[16,32,16,128]{3,1,0,2:T(8,128)(2,1)}), bf16[16,32,16,128]{3,1,0,2:T(8,128)(2,1)}, u32[]{:S(2)}, u32[]{:S(2)}) %all-to-all-start.1) | async-done | bytes 2097184 | tf_op jit(solution)/shard_map/all_to_all | solution.py:96
  132.7 2.4 copy.19
  135.1 3.9 fusion.17
  140.4 3.5 all-to-all-start.2
  145.3 7.3 %all-to-all-done.2 = bf16[32,32,2,128]{3,2,1,0:T(2,128)(2,1)S(1)} async-done(((bf16[32,32,2,128]{3,2,1,0:T(2,128)(2,1)}), bf16[32,32,2,128]{3,2,1,0:T(2,128)(2,1)S(1)}, u32[]{:S(2)}, u32[]{:S(2)}) %all-to-all-start.2) | async-done | bytes 524320 | tf_op jit(solution)/shard_map/all_to_all | solution.py:102
  152.7 13.9 %all-to-all-start.3 = ((bf16[32,32,2,128]{3,2,1,0:T(2,128)(2,1)}), bf16[32,32,2,128]{3,2,1,0:T(2,128)(2,1)S(1)}, u32[]{:S(2)}, u32[]{:S(2)}) async-start(bf16[32,32,2,128]{3,2,1,0:T(2,128)(2,1)} %copy.22), calls=%async_computation.3 | async-start | bytes 1048576 | tf_op jit(solution)/shard_map/all_to_all | solution.py:105
  166.9 8.1 %all-to-all-done.3 = bf16[32,32,2,128]{3,2,1,0:T(2,128)(2,1)S(1)} async-done(((bf16[32,32,2,128]{3,2,1,0:T(2,128)(2,1)}), bf16[32,32,2,128]{3,2,1,0:T(2,128)(2,1)S(1)}, u32[]{:S(2)}, u32[]{:S(2)}) %all-to-all-start.3) | async-done | bytes 524320 | tf_op jit(solution)/shard_map/all_to_all | solution.py:105
  175.8 8.2 %fusion.37 = f32[8,32,2,1,128]{4,3,2,1,0:T(1,128)S(1)} fusion(bf16[8,32,2,128,128]{4,3,2,1,0:T(8,128)(2,1)} %param.8, bf16[8,32,2,128,1]{3,1,2,0,4:T(8,128)(2,1)S(1)} %get-tuple-element.13), kind=kOutput, calls=%fused_computation.45 | convolution fusion | flops 16777216 | bytes 17170432 | tf_op jit(solution)/shard_map/abcd,abcde->abce/dot_general | solution.py:80
  184.1 8.2 %fusion.39 = f32[8,32,2,1,128]{4,3,2,1,0:T(1,128)S(1)} fusion(bf16[8,32,2,128,128]{4,3,2,1,0:T(8,128)(2,1)} %param.7, bf16[8,32,2,128,1]{3,1,2,0,4:T(8,128)(2,1)S(1)} %get-tuple-element.13), kind=kOutput, calls=%fused_computation.47 | convolution fusion | flops 16777216 | bytes 17170432 | tf_op jit(solution)/shard_map/abcd,abcde->abce/dot_general | solution.py:77
  192.3 4.4 %fusion.33 = f32[8,32,2,1,128]{4,3,2,1,0:T(1,128)S(1)} fusion(bf16[8,32,2,128,128]{4,3,2,1,0:T(8,128)(2,1)S(1)} %bitcast.98, bf16[8,32,2,128,1]{3,1,2,0,4:T(8,128)(2,1)S(1)} %get-tuple-element.14), kind=kOutput, calls=%fused_computation.41 | convolution fusion | flops 16777216 | bytes 17170432 | tf_op jit(solution)/shard_map/abcd,abcde->abce/dot_general | solution.py:82
  197.2 4.4 %fusion.35 = f32[8,32,2,1,128]{4,3,2,1,0:T(1,128)S(1)} fusion(bf16[8,32,2,128,128]{4,3,2,1,0:T(8,128)(2,1)S(1)} %bitcast.100, bf16[8,32,2,128,1]{3,1,2,0,4:T(8,128)(2,1)S(1)} %get-tuple-element.14), kind=kOutput, calls=%fused_computation.43 | convolution fusion | flops 16777216 | bytes 17170432 | tf_op jit(solution)/shard_map/abcd,abcde->abce/dot_general | solution.py:79
  205.1 3.5 all-to-all-start.4
  209.9 7.4 %all-to-all-done.4 = bf16[8,128,2,128]{3,2,0,1:T(2,128)(2,1)S(1)} async-done(((bf16[8,128,2,128]{3,2,0,1:T(2,128)(2,1)}), bf16[8,128,2,128]{3,2,0,1:T(2,128)(2,1)S(1)}, u32[]{:S(2)}, u32[]{:S(2)}) %all-to-all-start.4) | async-done | bytes 524320 | tf_op jit(solution)/shard_map/all_to_all | solution.py:117
  217.4 3.7 all-to-all-start.5
  221.2 8.6 %all-to-all-done.5 = bf16[8,128,2,128]{3,2,0,1:T(2,128)(2,1)S(1)} async-done(((bf16[8,128,2,128]{3,2,0,1:T(2,128)(2,1)}), bf16[8,128,2,128]{3,2,0,1:T(2,128)(2,1)S(1)}, u32[]{:S(2)}, u32[]{:S(2)}) %all-to-all-start.5) | async-done | bytes 524320 | tf_op jit(solution)/shard_map/all_to_all | solution.py:120
  230.0 3.8 convolution_convert_fusion
  235.6 3.5 copy.29
  239.1 3.6 all-to-all-start.6
  242.7 5.1 %copy.31 = bf16[128,32,2,128]{3,2,1,0:T(2,128)(2,1)} copy(bf16[128,32,2,128]{3,0,2,1:T(8,128)(2,1)} %get-tuple-element.6) | data formatting | bytes 4194304 | tf_op jit(solution)/shard_map/slice | solution.py:129
  247.8 43.0 %all-to-all-done.6 = bf16[128,32,2,128]{3,2,1,0:T(2,128)(2,1)S(1)} async-done(((bf16[128,32,2,128]{3,2,1,0:T(2,128)(2,1)}), bf16[128,32,2,128]{3,2,1,0:T(2,128)(2,1)S(1)}, u32[]{:S(2)}, u32[]{:S(2)}) %all-to-all-start.6) | async-done | bytes 2097184 | tf_op jit(solution)/shard_map/all_to_all | solution.py:128
  290.8 4.6 %all-to-all-start.7 = ((bf16[128,32,2,128]{3,2,1,0:T(2,128)(2,1)}), bf16[128,32,2,128]{3,2,1,0:T(2,128)(2,1)}, u32[]{:S(2)}, u32[]{:S(2)}) async-start(bf16[128,32,2,128]{3,2,1,0:T(2,128)(2,1)} %copy.31), calls=%async_computation.7 | async-start | bytes 4194304 | tf_op jit(solution)/shard_map/all_to_all | solution.py:129
  295.6 3.1 copy.30
  298.7 44.5 %all-to-all-done.7 = bf16[128,32,2,128]{3,2,1,0:T(2,128)(2,1)} async-done(((bf16[128,32,2,128]{3,2,1,0:T(2,128)(2,1)}), bf16[128,32,2,128]{3,2,1,0:T(2,128)(2,1)}, u32[]{:S(2)}, u32[]{:S(2)}) %all-to-all-start.7) | async-done | bytes 2097184 | tf_op jit(solution)/shard_map/all_to_all | solution.py:129
  343.2 4.4 %copy.32 = bf16[8,16,32,2,128]{4,3,0,2,1:T(2,128)(2,1)} copy(bf16[8,16,32,2,128]{4,3,2,1,0:T(2,128)(2,1)} %bitcast.40) | data formatting | bytes 4194304 | tf_op jit(solution)/shard_map/all_to_all | solution.py:129
  347.7 24.7 %fusion.13 = f32[256,16,32,128]{3,0,2,1:T(8,128)} fusion(bf16[16,32,16,128]{3,2,1,0:T(8,128)(2,1)} %bitcast.102, bf16[16,32,16,128]{3,2,1,0:T(8,128)(2,1)S(1)} %bitcast.101, bf16[16,256]{1,0:T(8,128)(2,1)S(1)} %get-tuple-element.18, bf16[16,256]{1,0:T(8,128)(2,1)S(1)} %get-tuple-element.17), kind=kOutput, calls=%fused_computation.15 | convolution fusion | flops 1082163200 | bytes 71319552 | tf_op jit(solution)/shard_map/xykc,kz->xyzc/dot_general | solution.py:131
  372.4 46.7 %fusion.7 = bf16[16,32,256,128]{3,2,1,0:T(8,128)(2,1)} fusion(f32[256,16,32,128]{3,0,2,1:T(8,128)} %fusion.13, f32[128]{0:T(128)S(1)} %convert_element_type.130, bf16[16,32,256,128]{3,2,1,0:T(8,128)(2,1)} %param.6, bf16[128,128]{1,0:T(8,128)(2,1)S(1)} %copy-done), kind=kOutput, calls=%fused_computation.8 | convolution fusion | flops 4479516672 | bytes 134251008 | tf_op jit(solution)/shard_map/xyzc,cd->xyzd/dot_general | solution.py:137
  (53 shorter events, 15.8 us)
Async XLA Ops:
  0.0 372.4 %copy-start = (bf16[128,128]{1,0:T(8,128)(2,1)S(1)}, bf16[128,128]{1,0:T(8,128)(2,1)}, u32[]{:S(2)}) copy-start(bf16[128,128]{1,0:T(8,128)(2,1)} %param.10) | copy-start | bytes 98308
  25.0 55.5 %all-to-all-start = ((bf16[16,32,16,128]{3,1,0,2:T(8,128)(2,1)}), bf16[16,32,16,128]{3,1,0,2:T(8,128)(2,1)S(1)}, u32[]{:S(2)}, u32[]{:S(2)}) async-start(bf16[16,32,16,128]{3,1,0,2:T(8,128)(2,1)} %copy.16), calls=%async_computation | async-start | bytes 4194304 | tf_op jit(solution)/shard_map/all_to_all | solution.py:95
  80.5 52.2 %all-to-all-start.1 = ((bf16[16,32,16,128]{3,1,0,2:T(8,128)(2,1)}), bf16[16,32,16,128]{3,1,0,2:T(8,128)(2,1)}, u32[]{:S(2)}, u32[]{:S(2)}) async-start(bf16[16,32,16,128]{3,1,0,2:T(8,128)(2,1)} %copy.18), calls=%async_computation.1 | async-start | bytes 4194304 | tf_op jit(solution)/shard_map/all_to_all | solution.py:96
  87.2 56.7 %copy-start.2 = (s32[8,2]{0,1:T(2,128)S(1)}, s32[8,2]{0,1:T(2,128)}, u32[]{:S(2)}) copy-start(s32[8,2]{0,1:T(2,128)} %param.9) | copy-start | bytes 196
  140.4 12.3 %all-to-all-start.2 = ((bf16[32,32,2,128]{3,2,1,0:T(2,128)(2,1)}), bf16[32,32,2,128]{3,2,1,0:T(2,128)(2,1)S(1)}, u32[]{:S(2)}, u32[]{:S(2)}) async-start(bf16[32,32,2,128]{3,2,1,0:T(2,128)(2,1)} %copy.20), calls=%async_computation.2 | async-start | bytes 1048576 | tf_op jit(solution)/shard_map/all_to_all | solution.py:102
  152.7 22.4 %all-to-all-start.3 = ((bf16[32,32,2,128]{3,2,1,0:T(2,128)(2,1)}), bf16[32,32,2,128]{3,2,1,0:T(2,128)(2,1)S(1)}, u32[]{:S(2)}, u32[]{:S(2)}) async-start(bf16[32,32,2,128]{3,2,1,0:T(2,128)(2,1)} %copy.22), calls=%async_computation.3 | async-start | bytes 1048576 | tf_op jit(solution)/shard_map/all_to_all | solution.py:105
  175.8 16.4 %slice-start = ((s8[16777216]{0:T(1024)(128)(4,1)}), s8[4194304]{0:T(1024)(128)(4,1)S(1)}, s32[]{:S(2)}) async-start(s8[16777216]{0:T(1024)(128)(4,1)} %bitcast.97), calls=%async_computation.8 | async-start | bytes 8388608
  175.8 16.4 %slice-start.1 = ((s8[16777216]{0:T(1024)(128)(4,1)}), s8[4194304]{0:T(1024)(128)(4,1)S(1)}, s32[]{:S(2)}) async-start(s8[16777216]{0:T(1024)(128)(4,1)} %bitcast.97), calls=%async_computation.9 | async-start | bytes 8388608
  184.0 8.2 %slice-start.2 = ((s8[16777216]{0:T(1024)(128)(4,1)}), s8[4194304]{0:T(1024)(128)(4,1)S(1)}, s32[]{:S(2)}) async-start(s8[16777216]{0:T(1024)(128)(4,1)} %bitcast.97), calls=%async_computation.10 | async-start | bytes 8388608
  184.0 8.2 %slice-start.3 = ((s8[16777216]{0:T(1024)(128)(4,1)}), s8[4194304]{0:T(1024)(128)(4,1)S(1)}, s32[]{:S(2)}) async-start(s8[16777216]{0:T(1024)(128)(4,1)} %bitcast.97), calls=%async_computation.11 | async-start | bytes 8388608
  184.0 12.7 %slice-start.4 = ((s8[16777216]{0:T(1024)(128)(4,1)}), s8[4194304]{0:T(1024)(128)(4,1)S(1)}, s32[]{:S(2)}) async-start(s8[16777216]{0:T(1024)(128)(4,1)} %bitcast.99), calls=%async_computation.12 | async-start | bytes 8388608
  184.0 12.7 %slice-start.5 = ((s8[16777216]{0:T(1024)(128)(4,1)}), s8[4194304]{0:T(1024)(128)(4,1)S(1)}, s32[]{:S(2)}) async-start(s8[16777216]{0:T(1024)(128)(4,1)} %bitcast.99), calls=%async_computation.13 | async-start | bytes 8388608
  192.3 4.5 %slice-start.6 = ((s8[16777216]{0:T(1024)(128)(4,1)}), s8[4194304]{0:T(1024)(128)(4,1)S(1)}, s32[]{:S(2)}) async-start(s8[16777216]{0:T(1024)(128)(4,1)} %bitcast.99), calls=%async_computation.14 | async-start | bytes 8388608
  192.3 4.9 %slice-start.7 = ((s8[16777216]{0:T(1024)(128)(4,1)}), s8[4194304]{0:T(1024)(128)(4,1)S(1)}, s32[]{:S(2)}) async-start(s8[16777216]{0:T(1024)(128)(4,1)} %bitcast.99), calls=%async_computation.15 | async-start | bytes 8388608
  205.1 12.3 %all-to-all-start.4 = ((bf16[8,128,2,128]{3,2,0,1:T(2,128)(2,1)}), bf16[8,128,2,128]{3,2,0,1:T(2,128)(2,1)S(1)}, u32[]{:S(2)}, u32[]{:S(2)}) async-start(bf16[8,128,2,128]{3,2,0,1:T(2,128)(2,1)} %copy.25), calls=%async_computation.4 | async-start | bytes 1048576 | tf_op jit(solution)/shard_map/all_to_all | solution.py:117
  217.4 12.5 %all-to-all-start.5 = ((bf16[8,128,2,128]{3,2,0,1:T(2,128)(2,1)}), bf16[8,128,2,128]{3,2,0,1:T(2,128)(2,1)S(1)}, u32[]{:S(2)}, u32[]{:S(2)}) async-start(bf16[8,128,2,128]{3,2,0,1:T(2,128)(2,1)} %copy.27), calls=%async_computation.5 | async-start | bytes 1048576 | tf_op jit(solution)/shard_map/all_to_all | solution.py:120
  235.6 59.9 %copy-start.3 = (bf16[128]{0:T(256)(128)(2,1)S(1)}, bf16[128]{0:T(256)(128)(2,1)}, u32[]{:S(2)}) copy-start(bf16[128]{0:T(256)(128)(2,1)} %param.11) | copy-start | bytes 772
  239.1 51.7 %all-to-all-start.6 = ((bf16[128,32,2,128]{3,2,1,0:T(2,128)(2,1)}), bf16[128,32,2,128]{3,2,1,0:T(2,128)(2,1)S(1)}, u32[]{:S(2)}, u32[]{:S(2)}) async-start(bf16[128,32,2,128]{3,2,1,0:T(2,128)(2,1)} %copy.29), calls=%async_computation.6 | async-start | bytes 4194304 | tf_op jit(solution)/shard_map/all_to_all | solution.py:128
  290.8 4.7 %copy-start.1 = (bf16[128,32,2,128]{3,2,1,0:T(2,128)(2,1)}, bf16[128,32,2,128]{3,2,1,0:T(2,128)(2,1)S(1)}, u32[]{:S(2)}) copy-start(bf16[128,32,2,128]{3,2,1,0:T(2,128)(2,1)S(1)} %all-to-all-done.6) | copy-start | bytes 6291460
  290.8 52.4 %all-to-all-start.7 = ((bf16[128,32,2,128]{3,2,1,0:T(2,128)(2,1)}), bf16[128,32,2,128]{3,2,1,0:T(2,128)(2,1)}, u32[]{:S(2)}, u32[]{:S(2)}) async-start(bf16[128,32,2,128]{3,2,1,0:T(2,128)(2,1)} %copy.31), calls=%async_computation.7 | async-start | bytes 4194304 | tf_op jit(solution)/shard_map/all_to_all | solution.py:129
where the time goes:
time: 423 us; the launch traced here: 419 us
  waiting for transfers between devices  209 us (49%)
  matrix products  125 us (30%)
  starting transfers between devices  44.3 us (10%)
  local copies, waits for them, and re-layouts  39.1 us (9%)
    dot_general x1, matrix products, per_device(): jnp.einsum('xyzc,cd->xyzd', grid_features, local_weight, preferred_elemen...  46.7 us
    all_to_all x1, waiting for transfers between devices, per_device(): lax.all_to_all(depth_imag, 'aa', split_axis=2, concat_axis=0, tiled=True)  45.5 us
    all_to_all x1, waiting for transfers between devices, per_device(): lax.all_to_all(depth_real, 'aa', split_axis=2, concat_axis=0, tiled=True)  44.8 us
    all_to_all x1, waiting for transfers between devices, per_device(): lax.all_to_all(result[NX:], 'aa', split_axis=0, concat_axis=2, tiled=True)  44.5 us
    all_to_all x1, waiting for transfers between devices, per_device(): lax.all_to_all(result[:NX], 'aa', split_axis=0, concat_axis=2, tiled=True)  43 us
    dot_general x1, matrix products, per_device(): jnp.einsum('xykc,kz->xyzc', jnp.concatenate(back_field, axis=2), inverse_...  24.7 us
    dot_general x1, matrix products, per_device(): jnp.einsum('xyzc,zk->xykc', grid_features, forward_depth, preferred_eleme...  18.5 us
    all_to_all x1, starting transfers between devices, per_device(): lax.all_to_all(result[KX:].astype(jnp.bfloat16), 'ba', split_axis=0, conc...  13.9 us
  transfers between devices with their start and end apart: 8, of which 8 were waited for; matrix products, arithmetic and copies ran while one was open for 4% of the time, Pallas kernels for 0%

commit v1 on v0

v1 whole, which is shorter than its diff:
```python
import functools
import math

import jax
import jax.numpy as jnp
from jax import lax
from jax.experimental import pallas as pl
from jax.experimental.pallas import tpu as pltpu
from jax.sharding import PartitionSpec as P

CHUNKS = 2
BF = jnp.bfloat16
F32 = jnp.float32


def kept_modes(length, number, positions):
    return jnp.where(positions < number // 2, positions, positions + (length - number))


def phase_tables(length, places, mode_list):
    phase_steps = places[:, None] * mode_list[None, :] % length
    angles = phase_steps.astype(F32) * (2.0 * math.pi / length)
    return jnp.cos(angles), jnp.sin(angles)


def forward_table(length, places, modes):
    c, s = phase_tables(length, places, modes)
    return jnp.stack([jnp.stack([c, -s], 1), jnp.stack([s, c], 1)], 0).astype(BF)


def inverse_table(length, places, modes):
    c, s = phase_tables(length, places, modes)
    c, s = c.T, s.T
    return jnp.stack([jnp.stack([c, s], 1), jnp.stack([-s, c], 1)], 0).astype(BF)


def depth_body(table_ref, x_ref, out_ref):
    rows = x_ref.shape[1]
    chans = x_ref.shape[3]
    for j in range(rows // 2):
        pair = jnp.concatenate([x_ref[0, 2 * j], x_ref[0, 2 * j + 1]], axis=1)
        res = jnp.dot(table_ref[...], pair, preferred_element_type=F32).astype(BF)
        out_ref[0, 2 * j] = res[:, :chans]
        out_ref[0, 2 * j + 1] = res[:, chans:]


def depth_forward(grid_features, table, first, count):
    _, rows, depth, chans = grid_features.shape
    modes = table.shape[0]
    return pl.pallas_call(
        depth_body,
        grid=(count,),
        in_specs=[
            pl.BlockSpec((modes, depth), lambda i: (0, 0)),
            pl.BlockSpec((1, rows, depth, chans), lambda i: (i + first, 0, 0, 0)),
        ],
        out_specs=pl.BlockSpec((1, rows, modes, chans), lambda i: (i, 0, 0, 0)),
        out_shape=jax.ShapeDtypeStruct((count, rows, modes, chans), BF),
        compiler_params=pltpu.CompilerParams(vmem_limit_bytes=24 << 20),
        cost_estimate=pl.CostEstimate(
            flops=2 * count * rows * depth * chans * modes * 16,
            bytes_accessed=2 * count * rows * depth * chans,
            transcendentals=0,
        ),
    )(table, grid_features)


def final_body(table_ref, w_ref, bias_ref, x_ref, back_ref, *rest):
    out_ref = rest[-1]
    bias = bias_ref[...]
    c1 = math.sqrt(2.0 / math.pi)

    for j in range(x_ref.shape[1]):
        val = jnp.dot(x_ref[0, j], w_ref[...], preferred_element_type=F32)
        val = val + jnp.dot(table_ref[...], back_ref[0, j], preferred_element_type=F32)
        val = val + bias
        inner = val * (c1 + (c1 * 0.044715) * (val * val))
        half = 0.5 * val
        out_ref[0, j] = (half + half * jnp.tanh(inner)).astype(BF)


def finish(grid_features, back, table, weight, bias, first, so_far):
    total, rows, depth, chans = grid_features.shape
    count, _, modes, _ = back.shape
    block = 8
    while rows % block:
        block //= 2
    big = pl.BlockSpec((1, block, depth, chans), lambda i, j: (i + first, j, 0, 0))
    in_specs = [
        pl.BlockSpec((depth, modes), lambda i, j: (0, 0)),
        pl.BlockSpec((chans, chans), lambda i, j: (0, 0)),
        pl.BlockSpec((1, chans), lambda i, j: (0, 0)),
        big,
        pl.BlockSpec((1, block, modes, chans), lambda i, j: (i, j, 0, 0)),
    ]
    operands = [table, weight, bias, grid_features, back]
    aliases = {}
    if so_far is not None:
        in_specs.append(pl.BlockSpec(memory_space=pl.ANY))
        operands.append(so_far)
        aliases = {5: 0}
    return pl.pallas_call(
        final_body,
        grid=(count, rows // block),
        in_specs=in_specs,
        out_specs=big,
        out_shape=jax.ShapeDtypeStruct(grid_features.shape, BF),
        input_output_aliases=aliases,
        compiler_params=pltpu.CompilerParams(vmem_limit_bytes=24 << 20),
        cost_estimate=pl.CostEstimate(
            flops=2 * count * rows * depth * chans * (chans + modes) * 8,
            bytes_accessed=4 * count * rows * depth * chans,
            transcendentals=count * rows * depth * chans,
        ),
    )(*operands)


def per_device(
    n_aa, n_ba, grid_features, weight_real, weight_imag, mode_keep, local_weight, local_bias
):
    n_x, n_y, depth, chans = grid_features.shape
    kx_own, ky, kz_own = weight_real.shape[:3]
    nx, ny = n_x * n_aa, n_y * n_ba
    kx, kz, ky_own = kx_own * n_ba, kz_own * n_aa, ky // n_ba
    bits = n_ba.bit_length() - 1
    me = lax.axis_index("ba")

    c, s = phase_tables(depth, jnp.arange(depth), jnp.arange(kz))
    depth_fwd = jnp.concatenate([c, -s], axis=1).T.astype(BF)
    factor = jnp.where(jnp.arange(kz) == 0, 1.0, 2.0).astype(F32) / (nx * ny * depth)
    depth_inv = jnp.concatenate([c * factor, -s * factor], axis=1).astype(BF)

    order = jnp.arange(n_ba)
    block = jnp.zeros_like(order)
    for bit in range(bits):
        block = block + ((order >> (bits - 1 - bit)) & 1) * (1 << bit)
    block = block ^ me
    ky_pos = (block[:, None] * ky_own + jnp.arange(ky_own)[None, :]).reshape(-1)
    ky_modes = kept_modes(ny, ky, ky_pos)
    own_y = me * n_y + jnp.arange(n_y)
    y_fwd = forward_table(ny, own_y, ky_modes)
    y_inv = inverse_table(ny, own_y, ky_modes)
    x_modes = kept_modes(nx, kx, jnp.arange(kx))
    x_fwd = forward_table(nx, jnp.arange(nx), x_modes)
    x_inv = inverse_table(nx, jnp.arange(nx), x_modes)

    def swap(value, bit):
        return lax.ppermute(value, "ba", [(i, i ^ (1 << bit)) for i in range(n_ba)])

    per = n_x // CHUNKS
    landed = []
    for ch in range(CHUNKS):
        coeffs = depth_forward(grid_features, depth_fwd, ch * per, per)
        coeffs = coeffs.reshape(per, n_y, 2, kz, chans)
        part = jnp.einsum("xypkc,pyrq->qrxkc", coeffs, y_fwd, preferred_element_type=F32)
        for bit in range(bits):
            half = part.shape[0] // 2
            got = swap(part[half:].astype(BF), bit)
            part = part[:half] + got.astype(F32)
        part = part.astype(BF).reshape(ky_own, 2, per, n_aa, kz_own, chans)
        part = jnp.transpose(part, (3, 2, 0, 1, 4, 5))
        landed.append(lax.all_to_all(part, "aa", 0, 0, tiled=True))
    field = jnp.stack(landed, 1).reshape(nx, ky_own, 2, kz_own, chans)
    spec = jnp.einsum("xqpkc,pxrm->mrqkc", field, x_fwd, preferred_element_type=F32).astype(BF)
    spec = spec.reshape(n_ba, kx_own, 2, ky_own, kz_own, chans)
    spec = lax.all_to_all(spec, "ba", 0, 0, tiled=True)
    spec = jnp.transpose(spec, (1, 0, 3, 4, 2, 5)).reshape(kx_own, ky, kz_own, 2, chans)

    pattern = "abcmd,abcde->abcme"
    by_real = jnp.einsum(pattern, spec, weight_real, preferred_element_type=F32)
    by_imag = jnp.einsum(pattern, spec, weight_imag, preferred_element_type=F32)
    out_real = by_real[..., 0, :] - by_imag[..., 1, :]
    out_imag = by_imag[..., 0, :] + by_real[..., 1, :]
    positions = jnp.arange(ky)
    levels = jnp.where(positions < ky // 2, positions, ky - 1 - positions)
    keep = (levels[None, :, None] < mode_keep[:, None, :]).astype(F32)[..., None]
    mixed = jnp.stack([out_real * keep, out_imag * keep], 0).astype(BF)
    mixed = mixed.reshape(2, kx_own, n_ba, ky_own, kz_own, chans)
    mixed = jnp.transpose(mixed, (2, 1, 0, 3, 4, 5))
    mixed = lax.all_to_all(mixed, "ba", 0, 0, tiled=True)
    mixed = mixed.reshape(kx, 2, ky_own, kz_own, chans)
    back = jnp.einsum("mpqkc,pmrx->xqrkc", mixed, x_inv, preferred_element_type=F32).astype(BF)
    back = back.reshape(n_aa, CHUNKS, per, ky_own, 2, kz_own, chans)

    bias = local_bias.astype(F32).reshape(1, chans)
    fields = []
    for ch in range(CHUNKS):
        piece = lax.all_to_all(back[:, ch], "aa", 0, 0, tiled=True)
        piece = jnp.transpose(piece, (2, 3, 1, 0, 4, 5))
        piece = piece.reshape(ky_own, 2, per, kz, chans)
        for bit in reversed(range(bits)):
            piece = jnp.concatenate([piece, swap(piece, bit)], axis=0)
        field = jnp.einsum("qpxkc,pqry->xyrkc", piece, y_inv, preferred_element_type=F32)
        fields.append(field.astype(BF).reshape(per, n_y, 2 * kz, chans))
    result = None
    for ch in range(CHUNKS):
        result = finish(
            grid_features, fields[ch], depth_inv, local_weight, bias, ch * per, result
        )
    return result


def solution(mesh):
    in_specs = (
        P("aa", "ba", None, None),
        P("ba", None, "aa", None, None),
        P("ba", None, "aa", None, None),
        P("ba", "aa"),
        P(),
        P(),
    )
    out_specs = P("aa", "ba", None, None)
    body = functools.partial(per_device, mesh.shape["aa"], mesh.shape["ba"])
    return jax.shard_map(body, mesh=mesh, in_specs=in_specs, out_specs=out_specs, check_vma=False)
```

time: 423 us -> 237 us (0.56)
  waiting for transfers between devices: 209 us -> 84.1 us
  matrix products: 125 us -> 22.5 us
  Pallas kernels: 0 us -> 78.2 us
  local copies, waits for them, and re-layouts: 39.1 us -> 10.9 us
  starting transfers between devices: 44.3 us -> 33.1 us
  other arithmetic: 0.73 us -> 5.58 us
    all_to_all x8 -> x6, waiting for transfers between devices: 209 us -> 50.6 us  [the longest x2 26.8 us: per_device(): piece = lax.all_to_all(back[:, ch], 'aa', 0, 0, tiled=True)]
    dot_general x11 -> x8, matrix products: 125 us -> 22.5 us  [the longest x1 8.05 us: per_device(): by_real = jnp.einsum(pattern, spec, weight_real, preferred_element_type=F32)]
    pallas_call x0 -> x4, Pallas kernels: none -> 78.2 us  [the longest x2 59.6 us: finish(): pl.pallas_call(final_body, grid=(count, rows // block), in_specs=in_specs...]
    ppermute x0 -> x8, waiting for transfers between devices: none -> 33.5 us  [swap(): return lax.ppermute(value, 'ba', [(i, i ^ 1 << bit) for i in range(n_ba)])]
    slice x13 -> x5, local copies, waits for them, and re-layouts: 25.9 us -> 0.96 us  [the longest x4 0.67 us: per_device(): got = swap(part[half:].astype(BF), bit)]
    all_to_all x8 -> x6, starting transfers between devices: 44.3 us -> 25.9 us  [the longest x2 11.7 us: per_device(): landed.append(lax.all_to_all(part, 'aa', 0, 0, tiled=True))]
    all_to_all x4 -> x0, local copies, waits for them, and re-layouts: 12.1 us -> none  [the longest x1 4.45 us: per_device(): lax.all_to_all(result[NX:], 'aa', split_axis=0, concat_axis=2, tiled=True)]
    ppermute x0 -> x8, starting transfers between devices: none -> 7.16 us  [swap(): return lax.ppermute(value, 'ba', [(i, i ^ 1 << bit) for i in range(n_ba)])]
  transfers between devices with their start and end apart: 8 -> 14, of which waited for: 8 -> 8; matrix products, arithmetic and copies ran while one was open for 4% -> 5% of each run, Pallas kernels for 0% -> 4%
where the time goes in v1:
time: 237 us; the launch traced here: 235 us
  waiting for transfers between devices  84.1 us (35%)
  Pallas kernels  78.2 us (33%)
  starting transfers between devices  33.1 us (14%)
  matrix products  22.5 us (9%)
  local copies, waits for them, and re-layouts  10.9 us (5%)
  other arithmetic  5.58 us (2%)
    pallas_call x2, Pallas kernels, finish(): pl.pallas_call(final_body, grid=(count, rows // block), in_specs=in_specs...  59.6 us
    ppermute x8, waiting for transfers between devices, swap(): return lax.ppermute(value, 'ba', [(i, i ^ 1 << bit) for i in range(n_ba)])  33.5 us
    all_to_all x2, waiting for transfers between devices, per_device(): piece = lax.all_to_all(back[:, ch], 'aa', 0, 0, tiled=True)  26.8 us
    pallas_call x2, Pallas kernels, depth_forward(): pl.pallas_call(depth_body, grid=(count,), in_specs=[pl.BlockSpec((modes,...  18.6 us
    all_to_all x2, waiting for transfers between devices, per_device(): landed.append(lax.all_to_all(part, 'aa', 0, 0, tiled=True))  12.1 us
    all_to_all x2, starting transfers between devices, per_device(): landed.append(lax.all_to_all(part, 'aa', 0, 0, tiled=True))  11.7 us
    dot_general x1, matrix products, per_device(): by_real = jnp.einsum(pattern, spec, weight_real, preferred_element_type=F32)  8.05 us
    dot_general x1, matrix products, per_device(): by_imag = jnp.einsum(pattern, spec, weight_imag, preferred_element_type=F32)  8.05 us
  transfers between devices with their start and end apart: 14, of which 8 were waited for; matrix products, arithmetic and copies ran while one was open for 5% of the time, Pallas kernels for 4%

profile of v1, /device:TPU:0, one launch (start us, length us, event | category | flops | bytes accessed | tf_op | source)
XLA Modules:
  0.0 234.8 jit_solution(5766569202670733205)
XLA Ops:
  0.5 9.3 %shard_map.64 = bf16[8,32,32,128]{3,2,1,0:T(8,128)(2,1)S(1)} custom-call(bf16[32,256]{1,0:T(8,128)(2,1)S(1)} %maximum_bitcast_fusion.25.table_ref, bf16[16,32,256,128]{3,2,1,0:T(8,128)(2,1)} %x_ref.7), custom_call_target="tpu_custom_call" | custom-call | flops 8589934592 | bytes 16777216 | tf_op jit(solution)/shard_map/pallas_call | solution.py:50
  11.5 9.3 %shard_map.65 = bf16[8,32,32,128]{3,2,1,0:T(8,128)(2,1)S(1)} custom-call(bf16[32,256]{1,0:T(8,128)(2,1)S(1)} %maximum_bitcast_fusion.25.table_ref, bf16[16,32,256,128]{3,2,1,0:T(8,128)(2,1)} %x_ref.7), custom_call_target="tpu_custom_call" | custom-call | flops 8589934592 | bytes 16777216 | tf_op jit(solution)/shard_map/pallas_call | solution.py:50
  21.7 2.0 copy-done.1
  24.5 3.0 %collective-permute-start.1 = (bf16[8,2,8,16,128]{4,0,3,2,1:T(8,128)(2,1)S(1)}, bf16[8,2,8,16,128]{4,0,3,2,1:T(8,128)(2,1)S(1)}, u32[]{:S(2)}, u32[]{:S(2)}) collective-permute-start(bf16[8,2,8,16,128]{4,0,3,2,1:T(8,128)(2,1)S(1)} %slice.93), channel_id=1, source_target_pairs={{0,2},{1,3},{2,0},{3,1},{4,6},{5,7},{6,4},{7,5},{8,10},{9,11},{10,... | collective-permute-start | bytes 1572872 | tf_op jit(solution)/shard_map/ppermute | solution.py:148
  27.5 12.1 %collective-permute-done.1 = bf16[8,2,8,16,128]{4,0,3,2,1:T(8,128)(2,1)S(1)} collective-permute-done((bf16[8,2,8,16,128]{4,0,3,2,1:T(8,128)(2,1)S(1)}, bf16[8,2,8,16,128]{4,0,3,2,1:T(8,128)(2,1)S(1)}, u32[]{:S(2)}, u32[]{:S(2)}) %collective-permute-start.1) | collective-permute-done | bytes 524320 | tf_op jit(solution)/shard_map/ppermute | solution.py:148
  39.8 0.9 copy.149
  40.6 6.0 %all-to-all-start = ((bf16[8,8,8,2,2,128]{5,2,4,1,3,0:T(8,128)(2,1)}), bf16[8,8,8,2,2,128]{5,2,4,1,3,0:T(8,128)(2,1)S(1)}, u32[]{:S(2)}, u32[]{:S(2)}) async-start(bf16[8,8,8,2,2,128]{5,2,4,1,3,0:T(8,128)(2,1)} %bitcast.149), calls=%async_computation | async-start | bytes 1048576 | tf_op jit(solution)/shard_map/all_to_all | solution.py:162
  46.7 1.9 slice_add_fusion
  48.6 1.6 collective-permute-start.3
  50.2 11.2 %collective-permute-done.3 = bf16[8,2,8,16,128]{4,0,3,2,1:T(8,128)(2,1)S(1)} collective-permute-done((bf16[8,2,8,16,128]{4,0,3,2,1:T(8,128)(2,1)S(1)}, bf16[8,2,8,16,128]{4,0,3,2,1:T(8,128)(2,1)S(1)}, u32[]{:S(2)}, u32[]{:S(2)}) %collective-permute-start.3) | collective-permute-done | bytes 524320 | tf_op jit(solution)/shard_map/ppermute | solution.py:148
  62.4 5.7 %all-to-all-start.1 = ((bf16[8,8,8,2,2,128]{5,2,4,1,3,0:T(8,128)(2,1)}), bf16[8,8,8,2,2,128]{5,2,4,1,3,0:T(8,128)(2,1)S(1)}, u32[]{:S(2)}, u32[]{:S(2)}) async-start(bf16[8,8,8,2,2,128]{5,2,4,1,3,0:T(8,128)(2,1)} %bitcast.148), calls=%async_computation.1 | async-start | bytes 1048576 | tf_op jit(solution)/shard_map/all_to_all | solution.py:162
  68.4 12.1 %all-to-all-done.1 = bf16[8,8,8,2,2,128]{5,2,4,1,3,0:T(8,128)(2,1)S(1)} async-done(((bf16[8,8,8,2,2,128]{5,2,4,1,3,0:T(8,128)(2,1)}), bf16[8,8,8,2,2,128]{5,2,4,1,3,0:T(8,128)(2,1)S(1)}, u32[]{:S(2)}, u32[]{:S(2)}) %all-to-all-start.1) | async-done | bytes 524320 | tf_op jit(solution)/shard_map/all_to_all | solution.py:162
  82.0 3.4 %all-to-all-start.2 = ((bf16[4,8,2,8,2,128]{5,1,4,3,2,0:T(8,128)(2,1)}), bf16[4,8,2,8,2,128]{5,1,4,3,2,0:T(8,128)(2,1)S(1)}, u32[]{:S(2)}, u32[]{:S(2)}) async-start(bf16[4,8,2,8,2,128]{5,1,4,3,2,0:T(8,128)(2,1)} %copy.80), calls=%async_computation.2 | async-start | bytes 524288 | tf_op jit(solution)/shard_map/all_to_all | solution.py:166
  85.5 5.9 %all-to-all-done.2 = bf16[4,8,2,8,2,128]{5,1,4,3,2,0:T(8,128)(2,1)S(1)} async-done(((bf16[4,8,2,8,2,128]{5,1,4,3,2,0:T(8,128)(2,1)}), bf16[4,8,2,8,2,128]{5,1,4,3,2,0:T(8,128)(2,1)S(1)}, u32[]{:S(2)}, u32[]{:S(2)}) %all-to-all-start.2) | async-done | bytes 262176 | tf_op jit(solution)/shard_map/all_to_all | solution.py:166
  91.6 8.0 %fusion.78 = f32[8,32,2,2,128]{4,3,2,1,0:T(2,128)S(1)} fusion(bf16[8,32,2,2,128]{4,3,2,1,0:T(2,128)(2,1)S(1)} %bitcast.156, bf16[8,32,2,128,128]{4,3,2,1,0:T(8,128)(2,1)} %param.8), kind=kOutput, calls=%fused_computation.160 | convolution fusion | flops 33554432 | bytes 17563648 | tf_op jit(solution)/shard_map/abcmd,abcde->abcme/dot_general | solution.py:171
  99.7 8.0 %fusion.77 = f32[8,32,2,2,128]{4,3,2,1,0:T(2,128)S(1)} fusion(bf16[8,32,2,2,128]{4,3,2,1,0:T(2,128)(2,1)S(1)} %bitcast.157, bf16[8,32,2,128,128]{4,3,2,1,0:T(8,128)(2,1)} %param.7), kind=kOutput, calls=%fused_computation.159 | convolution fusion | flops 33554432 | bytes 17563648 | tf_op jit(solution)/shard_map/abcmd,abcde->abcme/dot_general | solution.py:170
  108.5 0.9 copy.87
  109.4 3.4 %all-to-all-start.3 = ((bf16[4,8,2,8,2,128]{5,4,3,1,2,0:T(2,128)(2,1)}), bf16[4,8,2,8,2,128]{5,4,3,1,2,0:T(2,128)(2,1)S(1)}, u32[]{:S(2)}, u32[]{:S(2)}) async-start(bf16[4,8,2,8,2,128]{5,4,3,1,2,0:T(2,128)(2,1)} %copy.87), calls=%async_computation.3 | async-start | bytes 524288 | tf_op jit(solution)/shard_map/all_to_all | solution.py:180
  113.0 5.8 %all-to-all-done.3 = bf16[4,8,2,8,2,128]{5,4,3,1,2,0:T(2,128)(2,1)S(1)} async-done(((bf16[4,8,2,8,2,128]{5,4,3,1,2,0:T(2,128)(2,1)}), bf16[4,8,2,8,2,128]{5,4,3,1,2,0:T(2,128)(2,1)S(1)}, u32[]{:S(2)}, u32[]{:S(2)}) %all-to-all-start.3) | async-done | bytes 262176 | tf_op jit(solution)/shard_map/all_to_all | solution.py:180
  119.5 0.9 copy.147
  120.5 3.7 %all-to-all-start.4 = ((bf16[8,8,8,2,2,128]{5,1,4,2,3,0:T(8,128)(2,1)}), bf16[8,8,8,2,2,128]{5,1,4,2,3,0:T(8,128)(2,1)S(1)}, u32[]{:S(2)}, u32[]{:S(2)}) async-start(bf16[8,8,8,2,2,128]{5,1,4,2,3,0:T(8,128)(2,1)} %bitcast.147), calls=%async_computation.4 | async-start | bytes 1048576 | tf_op jit(solution)/shard_map/all_to_all | solution.py:188
  124.1 0.9 copy.146
  125.1 13.3 %all-to-all-done.4 = bf16[8,8,8,2,2,128]{5,1,4,2,3,0:T(8,128)(2,1)S(1)} async-done(((bf16[8,8,8,2,2,128]{5,1,4,2,3,0:T(8,128)(2,1)}), bf16[8,8,8,2,2,128]{5,1,4,2,3,0:T(8,128)(2,1)S(1)}, u32[]{:S(2)}, u32[]{:S(2)}) %all-to-all-start.4) | async-done | bytes 524320 | tf_op jit(solution)/shard_map/all_to_all | solution.py:188
  138.4 3.7 %all-to-all-start.5 = ((bf16[8,8,8,2,2,128]{5,1,4,2,3,0:T(8,128)(2,1)}), bf16[8,8,8,2,2,128]{5,1,4,2,3,0:T(8,128)(2,1)S(1)}, u32[]{:S(2)}, u32[]{:S(2)}) async-start(bf16[8,8,8,2,2,128]{5,1,4,2,3,0:T(8,128)(2,1)} %bitcast.146), calls=%async_computation.5 | async-start | bytes 1048576 | tf_op jit(solution)/shard_map/all_to_all | solution.py:188
  143.0 13.4 %all-to-all-done.5 = bf16[8,8,8,2,2,128]{5,1,4,2,3,0:T(8,128)(2,1)S(1)} async-done(((bf16[8,8,8,2,2,128]{5,1,4,2,3,0:T(8,128)(2,1)}), bf16[8,8,8,2,2,128]{5,1,4,2,3,0:T(8,128)(2,1)S(1)}, u32[]{:S(2)}, u32[]{:S(2)}) %all-to-all-start.5) | async-done | bytes 524320 | tf_op jit(solution)/shard_map/all_to_all | solution.py:188
  156.6 1.0 collective-permute-start.6
  157.6 1.2 pad_maximum_fusion.1
  158.8 10.2 %collective-permute-done.6 = bf16[8,2,8,16,128]{4,0,1,3,2:T(8,128)(2,1)S(1)} collective-permute-done((bf16[8,2,8,16,128]{4,0,1,3,2:T(8,128)(2,1)S(1)}, bf16[8,2,8,16,128]{4,0,1,3,2:T(8,128)(2,1)S(1)}, u32[]{:S(2)}, u32[]{:S(2)}) %collective-permute-start.6) | collective-permute-done | bytes 524320 | tf_op jit(solution)/shard_map/ppermute | solution.py:148
  169.5 2.0 fusion.12
  172.4 2.0 fusion.13
  175.2 29.8 %shard_map.66.rest_0_ = bf16[16,32,256,128]{3,2,1,0:T(8,128)(2,1)} custom-call(bf16[256,32]{1,0:T(8,128)(2,1)S(1)} %copy.98.table_ref, bf16[128,128]{1,0:T(8,128)(2,1)S(1)} %copy-done, f32[1,128]{1,0:T(1,128)S(1)} %bitcast_convert_fusion.3.bias_ref, bf16[16,32,256,128]{3,2,1,0:T(8,128)(2,1)} %x_ref.7, bf16[8,32,32,128]{3,2,1,0:T(8,128)(2,1)S(1)} %bitcast.153), custom_call_target="tpu_custom_call" | custom-call | flops 21474836480 | bytes 33554432 | tf_op jit(solution)/shard_map/pallas_call | solution.py:102
  205.0 29.8 %shard_map.67 = bf16[16,32,256,128]{3,2,1,0:T(8,128)(2,1)} custom-call(bf16[256,32]{1,0:T(8,128)(2,1)S(1)} %copy.98.table_ref, bf16[128,128]{1,0:T(8,128)(2,1)S(1)} %copy-done, f32[1,128]{1,0:T(1,128)S(1)} %bitcast_convert_fusion.3.bias_ref, bf16[16,32,256,128]{3,2,1,0:T(8,128)(2,1)} %x_ref.7, ...), custom_call_target="tpu_custom_call", output_to_operand_aliasing={{}: (5, {})} | custom-call | flops 21474836480 | bytes 33554432 | tf_op jit(solution)/shard_map/pallas_call | solution.py:102
  (65 shorter events, 11.8 us)
Async XLA Ops:
  10.9 13.1 %collective-permute-start = (bf16[16,2,8,16,128]{4,0,3,2,1:T(8,128)(2,1)S(1)}, bf16[16,2,8,16,128]{4,0,3,2,1:T(8,128)(2,1)S(1)}, u32[]{:S(2)}, u32[]{:S(2)}) collective-permute-start(bf16[16,2,8,16,128]{4,0,3,2,1:T(8,128)(2,1)S(1)} %slice.91), channel_id=1, source_target_pairs={{0,1},{1,0},{2,3},{3,2},{4,5},{5,4},{6,7},{7,6},{8,9},{9,8},{10,11... | collective-permute-start | bytes 3145736 | tf_op jit(solution)/shard_map/ppermute | solution.py:148
  21.6 2.0 copy-start.1
  23.9 22.7 %collective-permute-start.2 = (bf16[16,2,8,16,128]{4,0,3,2,1:T(8,128)(2,1)S(1)}, bf16[16,2,8,16,128]{4,0,3,2,1:T(8,128)(2,1)S(1)}, u32[]{:S(2)}, u32[]{:S(2)}) collective-permute-start(bf16[16,2,8,16,128]{4,0,3,2,1:T(8,128)(2,1)S(1)} %slice.90), channel_id=1, source_target_pairs={{0,1},{1,0},{2,3},{3,2},{4,5},{5,4},{6,7},{7,6},{8,9},{9,8},{10,11... | collective-permute-start | bytes 3145736 | tf_op jit(solution)/shard_map/ppermute | solution.py:148
  24.5 15.2 %collective-permute-start.1 = (bf16[8,2,8,16,128]{4,0,3,2,1:T(8,128)(2,1)S(1)}, bf16[8,2,8,16,128]{4,0,3,2,1:T(8,128)(2,1)S(1)}, u32[]{:S(2)}, u32[]{:S(2)}) collective-permute-start(bf16[8,2,8,16,128]{4,0,3,2,1:T(8,128)(2,1)S(1)} %slice.93), channel_id=1, source_target_pairs={{0,2},{1,3},{2,0},{3,1},{4,6},{5,7},{6,4},{7,5},{8,10},{9,11},{10,... | collective-permute-start | bytes 1572872 | tf_op jit(solution)/shard_map/ppermute | solution.py:148
  40.6 21.8 %all-to-all-start = ((bf16[8,8,8,2,2,128]{5,2,4,1,3,0:T(8,128)(2,1)}), bf16[8,8,8,2,2,128]{5,2,4,1,3,0:T(8,128)(2,1)S(1)}, u32[]{:S(2)}, u32[]{:S(2)}) async-start(bf16[8,8,8,2,2,128]{5,2,4,1,3,0:T(8,128)(2,1)} %bitcast.149), calls=%async_computation | async-start | bytes 1048576 | tf_op jit(solution)/shard_map/all_to_all | solution.py:162
  48.6 19.5 %copy-start.2 = (s32[8,2]{0,1:T(2,128)S(1)}, s32[8,2]{0,1:T(2,128)}, u32[]{:S(2)}) copy-start(s32[8,2]{0,1:T(2,128)} %param.9) | copy-start | bytes 196
  48.6 12.8 %collective-permute-start.3 = (bf16[8,2,8,16,128]{4,0,3,2,1:T(8,128)(2,1)S(1)}, bf16[8,2,8,16,128]{4,0,3,2,1:T(8,128)(2,1)S(1)}, u32[]{:S(2)}, u32[]{:S(2)}) collective-permute-start(bf16[8,2,8,16,128]{4,0,3,2,1:T(8,128)(2,1)S(1)} %slice.92), channel_id=1, source_target_pairs={{0,2},{1,3},{2,0},{3,1},{4,6},{5,7},{6,4},{7,5},{8,10},{9,11},{10,... | collective-permute-start | bytes 1572872 | tf_op jit(solution)/shard_map/ppermute | solution.py:148
  62.4 18.1 %all-to-all-start.1 = ((bf16[8,8,8,2,2,128]{5,2,4,1,3,0:T(8,128)(2,1)}), bf16[8,8,8,2,2,128]{5,2,4,1,3,0:T(8,128)(2,1)S(1)}, u32[]{:S(2)}, u32[]{:S(2)}) async-start(bf16[8,8,8,2,2,128]{5,2,4,1,3,0:T(8,128)(2,1)} %bitcast.148), calls=%async_computation.1 | async-start | bytes 1048576 | tf_op jit(solution)/shard_map/all_to_all | solution.py:162
  82.0 9.4 %all-to-all-start.2 = ((bf16[4,8,2,8,2,128]{5,1,4,3,2,0:T(8,128)(2,1)}), bf16[4,8,2,8,2,128]{5,1,4,3,2,0:T(8,128)(2,1)S(1)}, u32[]{:S(2)}, u32[]{:S(2)}) async-start(bf16[4,8,2,8,2,128]{5,1,4,3,2,0:T(8,128)(2,1)} %copy.80), calls=%async_computation.2 | async-start | bytes 524288 | tf_op jit(solution)/shard_map/all_to_all | solution.py:166
  109.4 9.4 %all-to-all-start.3 = ((bf16[4,8,2,8,2,128]{5,4,3,1,2,0:T(2,128)(2,1)}), bf16[4,8,2,8,2,128]{5,4,3,1,2,0:T(2,128)(2,1)S(1)}, u32[]{:S(2)}, u32[]{:S(2)}) async-start(bf16[4,8,2,8,2,128]{5,4,3,1,2,0:T(2,128)(2,1)} %copy.87), calls=%async_computation.3 | async-start | bytes 524288 | tf_op jit(solution)/shard_map/all_to_all | solution.py:180
  120.5 17.9 %all-to-all-start.4 = ((bf16[8,8,8,2,2,128]{5,1,4,2,3,0:T(8,128)(2,1)}), bf16[8,8,8,2,2,128]{5,1,4,2,3,0:T(8,128)(2,1)S(1)}, u32[]{:S(2)}, u32[]{:S(2)}) async-start(bf16[8,8,8,2,2,128]{5,1,4,2,3,0:T(8,128)(2,1)} %bitcast.147), calls=%async_computation.4 | async-start | bytes 1048576 | tf_op jit(solution)/shard_map/all_to_all | solution.py:188
  138.4 18.1 %all-to-all-start.5 = ((bf16[8,8,8,2,2,128]{5,1,4,2,3,0:T(8,128)(2,1)}), bf16[8,8,8,2,2,128]{5,1,4,2,3,0:T(8,128)(2,1)S(1)}, u32[]{:S(2)}, u32[]{:S(2)}) async-start(bf16[8,8,8,2,2,128]{5,1,4,2,3,0:T(8,128)(2,1)} %bitcast.146), calls=%async_computation.5 | async-start | bytes 1048576 | tf_op jit(solution)/shard_map/all_to_all | solution.py:188
  142.2 15.4 %collective-permute-start.4 = (bf16[8,2,8,16,128]{4,0,1,3,2:T(8,128)(2,1)S(1)}, bf16[8,2,8,16,128]{4,0,1,3,2:T(8,128)(2,1)S(1)}, u32[]{:S(2)}, u32[]{:S(2)}) collective-permute-start(bf16[8,2,8,16,128]{4,0,1,3,2:T(8,128)(2,1)S(1)} %bitcast.160), channel_id=1, source_target_pairs={{0,2},{1,3},{2,0},{3,1},{4,6},{5,7},{6,4},{7,5},{8,10},{9,11},{10,... | collective-permute-start | bytes 1572872 | tf_op jit(solution)/shard_map/ppermute | solution.py:148
  156.6 12.9 %copy-start.3 = (bf16[128]{0:T(256)(128)(2,1)S(1)}, bf16[128]{0:T(256)(128)(2,1)}, u32[]{:S(2)}) copy-start(bf16[128]{0:T(256)(128)(2,1)} %param.11) | copy-start | bytes 772
  156.6 12.4 %collective-permute-start.6 = (bf16[8,2,8,16,128]{4,0,1,3,2:T(8,128)(2,1)S(1)}, bf16[8,2,8,16,128]{4,0,1,3,2:T(8,128)(2,1)S(1)}, u32[]{:S(2)}, u32[]{:S(2)}) collective-permute-start(bf16[8,2,8,16,128]{4,0,1,3,2:T(8,128)(2,1)S(1)} %bitcast.163), channel_id=1, source_target_pairs={{0,2},{1,3},{2,0},{3,1},{4,6},{5,7},{6,4},{7,5},{8,10},{9,11},{10,... | collective-permute-start | bytes 1572872 | tf_op jit(solution)/shard_map/ppermute | solution.py:148
  158.8 10.8 %collective-permute-start.5 = (bf16[16,2,8,16,128]{4,0,1,3,2:T(8,128)(2,1)}, bf16[16,2,8,16,128]{4,0,1,3,2:T(8,128)(2,1)}, u32[]{:S(2)}, u32[]{:S(2)}) collective-permute-start(bf16[16,2,8,16,128]{4,0,1,3,2:T(8,128)(2,1)} %pad_maximum_fusion.1), channel_id=1, source_target_pairs={{0,1},{1,0},{2,3},{3,2},{4,5},{5,4},{6,7},{7,6},{8,9},{9,8},{10,11... | collective-permute-start | bytes 3145736 | tf_op jit(solution)/shard_map/ppermute | solution.py:148
  169.2 3.2 %collective-permute-start.7 = (bf16[16,2,8,16,128]{4,0,1,3,2:T(8,128)(2,1)S(1)}, bf16[16,2,8,16,128]{4,0,1,3,2:T(8,128)(2,1)}, u32[]{:S(2)}, u32[]{:S(2)}) collective-permute-start(bf16[16,2,8,16,128]{4,0,1,3,2:T(8,128)(2,1)S(1)} %pad_maximum_fusion.2), channel_id=1, source_target_pairs={{0,1},{1,0},{2,3},{3,2},{4,5},{5,4},{6,7},{7,6},{8,9},{9,8},{10,11... | collective-permute-start | bytes 3145736 | tf_op jit(solution)/shard_map/ppermute | solution.py:148
  174.3 0.8 copy-start
